TPU v7x, 256 devices: a whole 4x4x8 slice. The times are simulated.
256 devices in a mesh: gx: 16 (over z, core), gy: 4 (over x), gz: 4 (over y).
Axes of the slice: x: 4, y: 4, z: 8, core: 2. Of those that a mesh axis runs over, the one named last changes fastest.
Arguments:
- block_values: bfloat16 [4, 64, 4, 6, 128, 128], P('gy', 'gx', 'gz'), as said below
- block_cols: int32 [4, 64, 4, 6], P('gy', 'gx', 'gz'), may hold values from 0 to 63, as said below
Outputs:
- purified: float32 [2048, 32768], P(('gx', 'gy'), 'gz')
Inputs may be any that keep to these rules, and one draw needn't show every extreme that they name: block_cols[a, s, b, :] holds 6 distinct tile columns of panel b at which tile row a * 64 + s of P is nonzero; every tile column of a panel is listed by exactly 6 tile rows of each slab; the pattern is symmetric: tile (i, j) is listed exactly when tile (j, i) is. `block_values`: P is symmetric: the tile listed at (i, j) is the transpose of the tile listed at (j, i), and diagonal tiles are symmetric.
All inputs are finite; a program needn't handle non-finite values.
Results may differ from a plain program's by a relative error of at most 0.0033.
Values may be sent and summed in bfloat16 or wider, within the bound.
A program may use at most 128 MiB of HBM per device.

v0:
```python
import jax
import jax.numpy as jnp
from jax import lax
from jax.sharding import PartitionSpec as P

WIN = 1


def picked_2(x, axis, root):
    return lax.dynamic_index_in_dim(lax.all_gather(x, axis), root, 0, keepdims=False)


def in_blocks(x, dim, length):
    lengths = x.shape
    tiles = x.reshape(*lengths[:dim], length, lengths[dim] // length, *lengths[dim + 1 :])
    return jnp.moveaxis(tiles, dim, 0)


def sent_and_summed(x, axis, dim):
    tiles = in_blocks(x, dim, lax.axis_size(axis))
    arrived = lax.all_to_all(tiles, axis, split_axis=0, concat_axis=0, tiled=True)
    return arrived.astype(jnp.float32).sum(axis=0)


def densify(left_tiles, left_columns, slab_tiles):
    onehot = (
        left_columns[:, :, None] == jnp.arange(slab_tiles, dtype=jnp.int32)[None, None, :]
    ).astype(jnp.bfloat16)
    densified = jnp.einsum("wkj,wkyx->wyjx", onehot, left_tiles, preferred_element_type=jnp.float32)
    tile_size = left_tiles.shape[2]
    return densified.astype(jnp.bfloat16).reshape(
        left_tiles.shape[0] * tile_size, slab_tiles, tile_size
    )


def product_one(left_panel, panel_tiles, panel_columns):
    summed = jnp.zeros(
        (left_panel.shape[0], panel_tiles.shape[0], panel_tiles.shape[2]), jnp.float32
    )
    for column_slot in range(panel_tiles.shape[1]):
        picked = jnp.take(left_panel, panel_columns[:, column_slot], axis=1)
        summed = summed + jnp.einsum(
            "rix,iyx->riy", picked, panel_tiles[:, column_slot], preferred_element_type=jnp.float32
        )
    return summed


def product_two(rounded, panel_tiles, panel_columns, panel_width):
    summed = jnp.zeros((rounded.shape[0], panel_width, panel_tiles.shape[3]), jnp.float32)
    for column_slot in range(panel_tiles.shape[1]):
        product = jnp.einsum(
            "rix,ixy->riy", rounded, panel_tiles[:, column_slot], preferred_element_type=jnp.float32
        )
        summed = summed.at[:, panel_columns[:, column_slot], :].add(product)
    return summed


def local(block_values, block_cols):
    tiles_here = block_values[0, :, 0]
    columns_here = block_cols[0, :, 0]
    tile_size = tiles_here.shape[2]
    slab_tiles = tiles_here.shape[0] * lax.axis_size("gx")
    left_tiles, left_columns = (
        picked_2(tiles_here[:WIN], "gy", 0),
        picked_2(columns_here[:WIN], "gy", 0),
    )
    left_panel = densify(left_tiles, left_columns, slab_tiles)
    height = left_panel.shape[0]
    on_diagonal = (lax.axis_index("gy") == lax.axis_index("gz")).astype(jnp.float32)
    panel_tiles, panel_columns = (
        lax.all_gather(tiles_here, "gx", axis=0, tiled=True),
        lax.all_gather(columns_here, "gx", axis=0, tiled=True),
    )
    partial_square = product_one(left_panel, panel_tiles, panel_columns)
    partial_square = partial_square.reshape(height, slab_tiles * tile_size)
    square = lax.psum(partial_square, "gz")
    square_low = square.astype(jnp.bfloat16).reshape(height, slab_tiles, tile_size)
    applied = product_two(square_low, panel_tiles, panel_columns, slab_tiles).reshape(
        height // lax.axis_size("gy") * lax.axis_size("gy"), slab_tiles * tile_size
    )
    return sent_and_summed(
        (3.0 * on_diagonal * square - 2.0 * applied).astype(jnp.bfloat16), "gy", 0
    )


def solution(mesh):
    in_specs = (P("gy", "gx", "gz", None, None, None), P("gy", "gx", "gz", None))
    out_specs = P(("gx", "gy"), "gz")
    return jax.shard_map(local, mesh=mesh, in_specs=in_specs, out_specs=out_specs, check_vma=False)
```

profile of v0, /device:TPU:32, one launch (start us, length us, event | category | flops | bytes accessed | tf_op | source)
XLA Modules:
  0.0 381.8 jit_solution(5912386459244780532)
XLA Ops:
  8.8 9.7 %all-gather = s32[4,1,1,6]{3,2,1,0:T(1,128)S(1)} all-gather(s32[1,1,1,6]{3,2,1,0:T(1,128)S(1)} %slice-done.4), channel_id=2, replica_groups=mesh['gx'=16,'gy'=4,'gz'=4] {'gy'}, dimensions={0}, use_global_device_ids=true | all-gather | bytes 120 | tf_op jit(solution)/shard_map/all_gather | solution.py:10
  18.5 13.3 %all-gather.1 = bf16[4,1,1,6,128,128]{5,4,3,2,1,0:T(8,128)(2,1)S(1)} all-gather(bf16[1,1,1,6,128,128]{5,4,3,2,1,0:T(8,128)(2,1)S(1)} %slice-done.3), channel_id=3, replica_groups=mesh['gx'=16,'gy'=4,'gz'=4] {'gy'}, dimensions={0}, use_global_device_ids=true | all-gather | bytes 983040 | tf_op jit(solution)/shard_map/all_gather | solution.py:10
  34.1 18.6 %all-gather.2 = s32[1,64,1,6]{3,2,0,1:T(1,128)S(1)} all-gather(s32[1,4,1,6]{3,2,0,1:T(1,128)S(1)} %bitcast.101), channel_id=4, replica_groups=mesh['gx'=16,'gy'=4,'gz'=4] {'gx'}, dimensions={1}, use_global_device_ids=true | all-gather | bytes 1632 | tf_op jit(solution)/shard_map/all_gather | solution.py:72
  53.1 2.2 gather_fusion
  61.7 2.2 gather_fusion.1
  66.1 19.6 %all-gather.6.cloned.1.call-done = bf16[1,64,1,6,128,128]{5,4,1,3,2,0:T(8,128)(2,1)} async-done(((bf16[1,4,1,6,128,128]{5,4,1,3,2,0:T(8,128)(2,1)}), bf16[1,64,1,6,128,128]{5,4,1,3,2,0:T(8,128)(2,1)}) %all-gather.6.cloned.1.call-update) | async-done | bytes 12582928 | tf_op jit(solution)/shard_map/all_gather | solution.py:71
  85.7 6.2 %fusion.10 = f32[64,128,128]{1,2,0:T(8,128)} fusion(bf16[64,128,128]{2,1,0:T(8,128)(2,1)} %gather_fusion, pred[64]{0:T(512)(128)(4,1)S(1)} %get-tuple-element.29, bf16[64,6,128,128]{3,2,0,1:T(8,128)(2,1)} %bitcast.84), kind=kOutput, calls=%fused_computation.31 | convolution fusion | flops 269484032 | bytes 8388672 | tf_op jit(solution)/shard_map/rix,iyx->riy/dot_general | solution.py:42
  91.8 6.0 %fusion.2 = f32[64,128,128]{1,2,0:T(8,128)} fusion(bf16[64,128,128]{2,1,0:T(8,128)(2,1)} %gather_fusion.4, pred[64]{0:T(512)(128)(4,1)S(1)} %get-tuple-element.25, bf16[64,6,128,128]{3,2,0,1:T(8,128)(2,1)} %bitcast.85), kind=kOutput, calls=%fused_computation.23 | convolution fusion | flops 269484032 | bytes 8388672 | tf_op jit(solution)/shard_map/rix,iyx->riy/dot_general | solution.py:42
  97.8 3.6 fusion.4
  101.5 3.6 fusion.6
  105.1 3.6 fusion.8
  108.7 10.1 %add_add_fusion = f32[64,128,128]{1,2,0:T(8,128)} fusion(f32[64,128,128]{1,2,0:T(8,128)} %fusion.2, f32[64,128,128]{1,2,0:T(8,128)} %fusion.4, f32[64,128,128]{1,2,0:T(8,128)} %fusion.6, f32[64,128,128]{1,2,0:T(8,128)} %fusion.10, f32[64,128,128]{1,2,0:T(8,128)} %fusion.8, bf16[64,128,128]{2,1,0:T(8,128)(2,1)S(1)} %copy-done.4, ...), kind=kOutput, calls=%fused_computation.15 | convolution fusion | flops 274726912 | bytes 29360640 | tf_op jit(solution)/shard_map/rix,iyx->riy/dot_general | solution.py:42
  118.8 98.5 %all-reduce.2.cloned.1.call-done = f32[128,8192]{0,1:T(8,128)} async-done(((f32[128,8192]{0,1:T(8,128)}), f32[128,8192]{0,1:T(8,128)}) %all-reduce.2.cloned.1.call-update) | async-done | bytes 4194320 | tf_op jit(solution)/shard_map/psum | solution.py:76
  217.4 2.5 convert_element_type.27
  219.9 4.6 %fusion.24 = f32[64,128,128]{2,1,0:T(8,128)} fusion(bf16[128,64,128]{0,2,1:T(8,128)(2,1)S(1)} %bitcast.78, bf16[64,6,128,128]{3,2,0,1:T(8,128)(2,1)} %bitcast.86), kind=kOutput, calls=%fused_computation.47 | convolution fusion | flops 268435456 | bytes 8388608 | tf_op jit(solution)/shard_map/rix,ixy->riy/dot_general | solution.py:51
  224.5 4.6 %fusion.25 = f32[64,128,128]{2,1,0:T(8,128)} fusion(bf16[128,64,128]{0,2,1:T(8,128)(2,1)S(1)} %bitcast.79, bf16[64,6,128,128]{3,2,0,1:T(8,128)(2,1)} %bitcast.87), kind=kOutput, calls=%fused_computation.48 | convolution fusion | flops 268435456 | bytes 8388608 | tf_op jit(solution)/shard_map/rix,ixy->riy/dot_general | solution.py:51
  229.1 2.8 fusion.26
  231.9 2.8 fusion.27
  234.7 2.8 fusion.28
  237.5 2.8 fusion.29
  240.3 2.5 broadcast_in_dim.11
  242.8 13.7 %scatter_fusion = f32[128,64,128]{2,0,1:T(8,128)} fusion(f32[128,64,128]{2,0,1:T(8,128)} %broadcast_in_dim.11, s32[64]{0:T(128)S(1)} %get-tuple-element.7, f32[64,128,128]{2,1,0:T(8,128)} %fusion.24), kind=kCustom, calls=%fused_computation.6 | custom fusion | flops 1048576 | bytes 12583168 | tf_op jit(solution)/shard_map/scatter-add | solution.py:54
  256.5 13.7 %scatter_fusion.1 = f32[128,64,128]{2,0,1:T(8,128)} fusion(f32[128,64,128]{2,0,1:T(8,128)} %scatter_fusion, s32[64]{0:T(128)S(1)} %get-tuple-element.8, f32[64,128,128]{2,1,0:T(8,128)} %fusion.25), kind=kCustom, calls=%fused_computation.7 | custom fusion | flops 1048576 | bytes 12583168 | tf_op jit(solution)/shard_map/scatter-add | solution.py:54
  270.2 13.7 %scatter_fusion.2 = f32[128,64,128]{2,0,1:T(8,128)} fusion(f32[128,64,128]{2,0,1:T(8,128)} %scatter_fusion.1, s32[64]{0:T(128)S(1)} %get-tuple-element.9, f32[64,128,128]{2,1,0:T(8,128)} %fusion.26), kind=kCustom, calls=%fused_computation.8 | custom fusion | flops 1048576 | bytes 12583168 | tf_op jit(solution)/shard_map/scatter-add | solution.py:54
  283.9 13.6 %scatter_fusion.3 = f32[128,64,128]{2,0,1:T(8,128)} fusion(f32[128,64,128]{2,0,1:T(8,128)} %scatter_fusion.2, s32[64]{0:T(128)S(1)} %get-tuple-element.10, f32[64,128,128]{2,1,0:T(8,128)} %fusion.27), kind=kCustom, calls=%fused_computation.9 | custom fusion | flops 1048576 | bytes 12583168 | tf_op jit(solution)/shard_map/scatter-add | solution.py:54
  297.5 13.7 %scatter_fusion.4 = f32[128,64,128]{2,0,1:T(8,128)} fusion(f32[128,64,128]{2,0,1:T(8,128)} %scatter_fusion.3, s32[64]{0:T(128)S(1)} %get-tuple-element.11, f32[64,128,128]{2,1,0:T(8,128)} %fusion.28), kind=kCustom, calls=%fused_computation.10 | custom fusion | flops 1048576 | bytes 12583168 | tf_op jit(solution)/shard_map/scatter-add | solution.py:54
  311.1 13.6 %scatter_fusion.5 = f32[128,64,128]{2,0,1:T(8,128)} fusion(f32[128,64,128]{2,0,1:T(8,128)} %scatter_fusion.4, s32[64]{0:T(128)S(1)} %get-tuple-element.6, f32[64,128,128]{2,1,0:T(8,128)} %fusion.29), kind=kCustom, calls=%fused_computation.11 | custom fusion | flops 1048576 | bytes 12583168 | tf_op jit(solution)/shard_map/scatter-add | solution.py:54
  324.8 4.7 %broadcast_multiply_fusion = f32[128,64,128]{2,0,1:T(8,128)} fusion(f32[128,64,128]{2,0,1:T(8,128)} %scatter_fusion.5), kind=kLoop, calls=%fused_computation.39 | loop fusion | flops 1048576 | bytes 8388608 | tf_op jit(solution)/shard_map/mul | solution.py:82
  329.5 5.6 %copy.42 = f32[128,64,128]{0,2,1:T(8,128)} copy(f32[128,64,128]{2,0,1:T(8,128)} %broadcast_multiply_fusion) | data formatting | bytes 8388608 | tf_op jit(solution)/shard_map/mul | solution.py:82
  335.1 5.2 %fusion = bf16[128,8192]{0,1:T(8,128)(2,1)} fusion(f32[128,64,128]{0,2,1:T(8,128)} %copy.42, f32[128,8192]{0,1:T(8,128)} %all-reduce.2.cloned.1.call-done, f32[]{:T(128)S(6)} %mul_shard_map.3), kind=kLoop, calls=%fused_computation.13 | loop fusion | flops 3145728 | bytes 10485764 | tf_op jit(solution)/shard_map/convert_element_type | solution.py:82
  340.3 2.9 copy.43
  343.3 30.4 %all_to_all.5 = bf16[4,32,8192]{2,1,0:T(8,128)(2,1)S(1)} all-to-all(bf16[4,32,8192]{2,1,0:T(8,128)(2,1)S(1)} %bitcast.99), channel_id=1, replica_groups=mesh['gx'=16,'gy'=4,'gz'=4] {'gy'}, dimensions={0} | all-to-all | bytes 4194304 | tf_op jit(solution)/shard_map/all_to_all | solution.py:21
  (50 shorter events, 14.8 us)
Async XLA Ops:
  6.5 12.0 %slice-start.3 = ((bf16[1,4,1,6,128,128]{5,4,3,2,1,0:T(8,128)(2,1)}), bf16[1,1,1,6,128,128]{5,4,3,2,1,0:T(8,128)(2,1)S(1)}, s32[]{:S(2)}) async-start(bf16[1,4,1,6,128,128]{5,4,3,2,1,0:T(8,128)(2,1)} %param.4), calls=%async_computation.6 | async-start | bytes 393216 | tf_op jit(solution)/shard_map/slice | solution.py:64
  6.5 2.2 slice-start.4
  6.5 79.1 %all-gather.6.cloned.1.call-start = ((), (), s32[]{:S(2)}) async-start(), calls=%async_computation.2 | async-start | bytes 13369344 | tf_op jit(solution)/shard_map/all_gather | solution.py:71
  8.7 208.6 %all-reduce.2.cloned.1.call-start = ((), (), s32[]{:S(2)}) async-start(), calls=%async_computation.1 | async-start | bytes 8388608 | tf_op jit(solution)/shard_map/psum | solution.py:76
  32.7 1.4 copy-start.5
  85.7 12.2 %copy-start = (bf16[1,64,1,6,128,128]{5,4,1,3,2,0:T(8,128)(2,1)S(1)}, bf16[1,64,1,6,128,128]{5,4,1,3,2,0:T(8,128)(2,1)}, u32[]{:S(2)}) copy-start(bf16[1,64,1,6,128,128]{5,4,1,3,2,0:T(8,128)(2,1)} %all-gather.6.cloned.1.call-done) | copy-start | bytes 37748740
  91.8 6.0 %copy-start.1 = (bf16[64,128,128]{2,1,0:T(8,128)(2,1)S(1)}, bf16[64,128,128]{2,1,0:T(8,128)(2,1)}, u32[]{:S(2)}) copy-start(bf16[64,128,128]{2,1,0:T(8,128)(2,1)} %gather_fusion.3) | copy-start | bytes 6291460
  97.8 3.6 copy-start.2
  101.5 3.6 copy-start.3
  105.1 3.6 copy-start.4
  217.4 11.7 %slice-start = ((s8[12582912]{0:T(1024)(128)(4,1)}), s8[4194304]{0:T(1024)(128)(4,1)S(1)}, s32[]{:S(2)}) async-start(s8[12582912]{0:T(1024)(128)(4,1)} %bitcast.92), calls=%async_computation.3 | async-start | bytes 8388608
  219.9 9.2 %slice-start.1 = ((s8[12582912]{0:T(1024)(128)(4,1)}), s8[4194304]{0:T(1024)(128)(4,1)S(1)}, s32[]{:S(2)}) async-start(s8[12582912]{0:T(1024)(128)(4,1)} %bitcast.92), calls=%async_computation.4 | async-start | bytes 8388608
  224.5 4.6 %slice-start.2 = ((s8[12582912]{0:T(1024)(128)(4,1)}), s8[4194304]{0:T(1024)(128)(4,1)S(1)}, s32[]{:S(2)}) async-start(s8[12582912]{0:T(1024)(128)(4,1)} %bitcast.92), calls=%async_computation.5 | async-start | bytes 8388608
Sparse Core Ops, SparseCore 0:
  9.2 76.4 all-gather.5
  118.9 98.3 all-reduce.1
where the time goes:
time: 383 us; the launch traced here: 382 us
  waiting for transfers between devices  118 us (31%)
  other arithmetic  96.3 us (25%)
  blocking collectives  72 us (19%)
  matrix products  54.3 us (14%)
  local copies, waits for them, and re-layouts  27.4 us (7%)
  between operations  13.5 us (4%)
    psum x1, waiting for transfers between devices, local(): square = lax.psum(partial_square, 'gz')  98.5 us
    scatter-add x6, other arithmetic, product_two(): summed = summed.at[:, panel_columns[:, column_slot], :].add(product)  82 us
    dot_general x6, matrix products, product_one(): jnp.einsum('rix,iyx->riy', picked, panel_tiles[:, column_slot], preferred...  33.1 us
    all_to_all x1, blocking collectives, sent_and_summed(): lax.all_to_all(tiles, axis, split_axis=0, concat_axis=0, tiled=True)  30.4 us
    all_gather x2, blocking collectives, picked_2(): lax.all_gather(x, axis)  23 us
    dot_general x6, matrix products, product_two(): jnp.einsum('rix,ixy->riy', rounded, panel_tiles[:, column_slot], preferre...  20.4 us
    all_gather x1, waiting for transfers between devices, local(): lax.all_gather(tiles_here, 'gx', axis=0, tiled=True)  19.6 us
    all_gather x1, blocking collectives, local(): lax.all_gather(columns_here, 'gx', axis=0, tiled=True)  18.6 us
  transfers between devices with their start and end apart: 2, of which 2 were waited for; matrix products, arithmetic and copies ran while one was open for 4% of the time, Pallas kernels for 0%

commit v1 on v0

--- a/solution.py
+++ b/solution.py
@@ -4,6 +4,12 @@
 from jax.sharding import PartitionSpec as P
 
 WIN = 1
+
+
+def gather_by_exchange(x, axis, dim):
+    size = lax.axis_size(axis)
+    repeats = [size if d == dim else 1 for d in range(x.ndim)]
+    return lax.all_to_all(jnp.tile(x, repeats), axis, split_axis=dim, concat_axis=dim, tiled=True)
 
 
 def picked_2(x, axis, root):
@@ -68,7 +74,7 @@
     height = left_panel.shape[0]
     on_diagonal = (lax.axis_index("gy") == lax.axis_index("gz")).astype(jnp.float32)
     panel_tiles, panel_columns = (
-        lax.all_gather(tiles_here, "gx", axis=0, tiled=True),
+        gather_by_exchange(tiles_here, "gx", 0),
         lax.all_gather(columns_here, "gx", axis=0, tiled=True),
     )
     partial_square = product_one(left_panel, panel_tiles, panel_columns)

time: 383 us -> 621 us (1.62)
  blocking collectives: 72 us -> 310 us
  waiting for transfers between devices: 118 us -> 99.3 us
  starting transfers between devices: 0.04 us -> 8.75 us
  local copies, waits for them, and re-layouts: 27.4 us -> 35.1 us
    all_gather x1, blocking collectives: 18.6 us -> 256 us  [local(): lax.all_gather(columns_here, 'gx', axis=0, tiled=True)]
    all_gather x1 -> x0, waiting for transfers between devices: 19.6 us -> none  [local(): lax.all_gather(tiles_here, 'gx', axis=0, tiled=True)]
    another operation x0 -> x1, local copies, waits for them, and re-layouts: none -> 8.82 us  [gather_by_exchange(): jnp.tile(x, repeats)]
    all_to_all x0 -> x1, starting transfers between devices: none -> 8.72 us  [gather_by_exchange(): lax.all_to_all(jnp.tile(x, repeats), axis, split_axis=dim, concat_axis=di...]
  transfers between devices with their start and end apart: 2 -> 2, of which waited for: 2 -> 1; matrix products, arithmetic and copies ran while one was open for 4% -> 3% of each run, Pallas kernels for 0% -> 0%
where the time goes in v1:
time: 621 us; the launch traced here: 620 us
  blocking collectives  310 us (50%)
  waiting for transfers between devices  99.3 us (16%)
  other arithmetic  96.4 us (16%)
  matrix products  56.8 us (9%)
  local copies, waits for them, and re-layouts  35.1 us (6%)
  between operations  13.6 us (2%)
  starting transfers between devices  8.75 us (1%)
    all_gather x1, blocking collectives, local(): lax.all_gather(columns_here, 'gx', axis=0, tiled=True)  256 us
    psum x1, waiting for transfers between devices, local(): square = lax.psum(partial_square, 'gz')  99.3 us
    scatter-add x6, other arithmetic, product_two(): summed = summed.at[:, panel_columns[:, column_slot], :].add(product)  82.3 us
    all_to_all x1, blocking collectives, sent_and_summed(): lax.all_to_all(tiles, axis, split_axis=0, concat_axis=0, tiled=True)  30 us
    dot_general x6, matrix products, product_one(): jnp.einsum('rix,iyx->riy', picked, panel_tiles[:, column_slot], preferred...  29.6 us
    dot_general x6, matrix products, product_two(): jnp.einsum('rix,ixy->riy', rounded, panel_tiles[:, column_slot], preferre...  26.3 us
    all_gather x2, blocking collectives, picked_2(): lax.all_gather(x, axis)  23.7 us
    gather x6, local copies, waits for them, and re-layouts, product_one(): picked = jnp.take(left_panel, panel_columns[:, column_slot], axis=1)  12.9 us
  transfers between devices with their start and end apart: 2, of which 1 were waited for; matrix products, arithmetic and copies ran while one was open for 3% of the time, Pallas kernels for 0%

profile of v1, /device:TPU:32, one launch (start us, length us, event | category | flops | bytes accessed | tf_op | source)
XLA Modules:
  0.0 619.6 jit_solution(15630794862738572767)
XLA Ops:
  6.5 8.8 %tile.11 = bf16[16,4,6,128,128]{4,3,2,1,0:T(8,128)(2,1)} broadcast(bf16[4,6,128,128]{3,2,1,0:T(8,128)(2,1)} %bitcast.101), dimensions={1,2,3,4} | broadcast | bytes 13369344 | tf_op jit(solution)/shard_map/tile | solution.py:12
  15.4 8.7 %all-to-all-start = ((bf16[64,6,128,128]{3,2,1,0:T(8,128)(2,1)}), bf16[64,6,128,128]{3,2,1,0:T(8,128)(2,1)}, u32[]{:S(2)}, u32[]{:S(2)}) async-start(bf16[64,6,128,128]{3,2,1,0:T(8,128)(2,1)} %bitcast.97), calls=%async_computation | async-start | bytes 25165824 | tf_op jit(solution)/shard_map/all_to_all | solution.py:12
  24.1 9.7 %all-gather = s32[4,1,1,6]{3,2,1,0:T(1,128)S(1)} all-gather(s32[1,1,1,6]{3,2,1,0:T(1,128)S(1)} %slice-done), channel_id=2, replica_groups=mesh['gx'=16,'gy'=4,'gz'=4] {'gy'}, dimensions={0}, use_global_device_ids=true | all-gather | bytes 120 | tf_op jit(solution)/shard_map/all_gather | solution.py:16
  34.8 13.9 %all-gather.1 = bf16[4,1,1,6,128,128]{5,4,3,2,1,0:T(8,128)(2,1)S(1)} all-gather(bf16[1,1,1,6,128,128]{5,4,3,2,1,0:T(8,128)(2,1)S(1)} %slice.59), channel_id=3, replica_groups=mesh['gx'=16,'gy'=4,'gz'=4] {'gy'}, dimensions={0}, use_global_device_ids=true | all-gather | bytes 983040 | tf_op jit(solution)/shard_map/all_gather | solution.py:16
  51.0 256.0 %all-gather.2 = s32[1,64,1,6]{3,2,0,1:T(1,128)S(1)} all-gather(s32[1,4,1,6]{3,2,0,1:T(1,128)S(1)} %bitcast.102), channel_id=4, replica_groups=mesh['gx'=16,'gy'=4,'gz'=4] {'gx'}, dimensions={1}, use_global_device_ids=true | all-gather | bytes 1632 | tf_op jit(solution)/shard_map/all_gather | solution.py:78
  318.2 2.2 gather_fusion.5
  320.5 4.0 fusion.10
  324.5 3.4 fusion.2
  327.9 3.4 fusion.4
  331.4 5.3 fusion.6
  336.7 5.4 fusion.8
  342.0 8.1 %add_add_fusion = f32[64,128,128]{1,2,0:T(8,128)} fusion(f32[64,128,128]{1,2,0:T(8,128)S(1)} %fusion.2, f32[64,128,128]{1,2,0:T(8,128)S(1)} %fusion.4, f32[64,128,128]{1,2,0:T(8,128)} %fusion.6, f32[64,128,128]{1,2,0:T(8,128)S(1)} %fusion.10, f32[64,128,128]{1,2,0:T(8,128)} %fusion.8, bf16[64,128,128]{2,1,0:T(8,128)(2,1)S(1)} %copy-done.4, ...), kind=kOutput, calls=%fused_computation.15 | convolution fusion | flops 274726912 | bytes 29360192 | tf_op jit(solution)/shard_map/rix,iyx->riy/dot_general | solution.py:48
  350.2 99.3 %all-reduce.2.cloned.1.call-done = f32[128,8192]{0,1:T(8,128)} async-done(((f32[128,8192]{0,1:T(8,128)}), f32[128,8192]{0,1:T(8,128)}) %all-reduce.2.cloned.1.call-update) | async-done | bytes 4194320 | tf_op jit(solution)/shard_map/psum | solution.py:82
  449.5 2.4 convert_element_type.27
  451.9 4.4 fusion.24
  456.3 2.5 broadcast_in_dim.11
  458.7 13.9 %scatter_fusion = f32[128,64,128]{2,0,1:T(8,128)} fusion(f32[128,64,128]{2,0,1:T(8,128)} %broadcast_in_dim.11, s32[64]{0:T(128)S(1)} %get-tuple-element.7, f32[64,128,128]{2,1,0:T(8,128)} %fusion.24), kind=kCustom, calls=%fused_computation.6 | custom fusion | flops 1048576 | bytes 12583168 | tf_op jit(solution)/shard_map/scatter-add | solution.py:60
  472.6 4.4 fusion.25
  477.0 13.7 %scatter_fusion.1 = f32[128,64,128]{2,0,1:T(8,128)} fusion(f32[128,64,128]{2,0,1:T(8,128)} %scatter_fusion, s32[64]{0:T(128)S(1)} %get-tuple-element.8, f32[64,128,128]{2,1,0:T(8,128)} %fusion.25), kind=kCustom, calls=%fused_computation.7 | custom fusion | flops 1048576 | bytes 12583168 | tf_op jit(solution)/shard_map/scatter-add | solution.py:60
  490.7 4.4 fusion.26
  495.1 13.7 %scatter_fusion.2 = f32[128,64,128]{2,0,1:T(8,128)} fusion(f32[128,64,128]{2,0,1:T(8,128)} %scatter_fusion.1, s32[64]{0:T(128)S(1)} %get-tuple-element.9, f32[64,128,128]{2,1,0:T(8,128)} %fusion.26), kind=kCustom, calls=%fused_computation.8 | custom fusion | flops 1048576 | bytes 12583168 | tf_op jit(solution)/shard_map/scatter-add | solution.py:60
  508.8 4.4 fusion.27
  513.2 13.6 %scatter_fusion.3 = f32[128,64,128]{2,0,1:T(8,128)} fusion(f32[128,64,128]{2,0,1:T(8,128)} %scatter_fusion.2, s32[64]{0:T(128)S(1)} %get-tuple-element.10, f32[64,128,128]{2,1,0:T(8,128)} %fusion.27), kind=kCustom, calls=%fused_computation.9 | custom fusion | flops 1048576 | bytes 12583168 | tf_op jit(solution)/shard_map/scatter-add | solution.py:60
  526.8 4.4 fusion.28
  531.2 13.8 %scatter_fusion.4 = f32[128,64,128]{2,0,1:T(8,128)} fusion(f32[128,64,128]{2,0,1:T(8,128)} %scatter_fusion.3, s32[64]{0:T(128)S(1)} %get-tuple-element.11, f32[64,128,128]{2,1,0:T(8,128)} %fusion.28), kind=kCustom, calls=%fused_computation.10 | custom fusion | flops 1048576 | bytes 12583168 | tf_op jit(solution)/shard_map/scatter-add | solution.py:60
  545.0 4.4 fusion.29
  549.4 13.6 %scatter_fusion.5 = f32[128,64,128]{2,0,1:T(8,128)} fusion(f32[128,64,128]{2,0,1:T(8,128)} %scatter_fusion.4, s32[64]{0:T(128)S(1)} %get-tuple-element.6, f32[64,128,128]{2,1,0:T(8,128)} %fusion.29), kind=kCustom, calls=%fused_computation.11 | custom fusion | flops 1048576 | bytes 12583168 | tf_op jit(solution)/shard_map/scatter-add | solution.py:60
  563.0 4.7 broadcast_multiply_fusion
  567.7 5.6 copy.47
  573.3 5.2 fusion
  578.5 2.9 copy.48
  581.4 30.0 %all_to_all.10 = bf16[4,32,8192]{2,1,0:T(8,128)(2,1)S(1)} all-to-all(bf16[4,32,8192]{2,1,0:T(8,128)(2,1)S(1)} %bitcast.99), channel_id=1, replica_groups=mesh['gx'=16,'gy'=4,'gz'=4] {'gy'}, dimensions={0} | all-to-all | bytes 4194304 | tf_op jit(solution)/shard_map/all_to_all | solution.py:27
  (41 shorter events, 15.7 us)
Async XLA Ops:
  15.4 8.8 %slice-start = ((s32[1,4,1,6]{3,2,1,0:T(1,128)}), s32[1,1,1,6]{3,2,1,0:T(1,128)S(1)}, s32[]{:S(2)}) async-start(s32[1,4,1,6]{3,2,1,0:T(1,128)} %param.5), calls=%async_computation.3 | async-start | bytes 1024 | tf_op jit(solution)/shard_map/slice | solution.py:71
  15.4 305.1 %all-to-all-start = ((bf16[64,6,128,128]{3,2,1,0:T(8,128)(2,1)}), bf16[64,6,128,128]{3,2,1,0:T(8,128)(2,1)}, u32[]{:S(2)}, u32[]{:S(2)}) async-start(bf16[64,6,128,128]{3,2,1,0:T(8,128)(2,1)} %bitcast.97), calls=%async_computation | async-start | bytes 25165824 | tf_op jit(solution)/shard_map/all_to_all | solution.py:12
  24.1 425.4 %all-reduce.2.cloned.1.call-start = ((), (), s32[]{:S(2)}) async-start(), calls=%async_computation.2 | async-start | bytes 8388608 | tf_op jit(solution)/shard_map/psum | solution.py:82
  49.6 1.4 copy-start.5
  320.5 4.0 copy-start
  324.5 3.4 copy-start.1
  327.9 3.4 copy-start.2
  331.3 5.3 copy-start.3
  336.7 5.4 copy-start.4
Sparse Core Ops, SparseCore 0:
  350.3 99.1 all-reduce.1
